TPU v7x, 32 devices: a 4x4x1 block of a 4x4x8 slice. The times are simulated.
32 devices in a mesh: dp: 1 (over z), ep_b: 4 (over y), ep_a: 8 (over x, core).
Axes of the slice: x: 4, y: 4, z: 1, core: 2. Of those that a mesh axis runs over, the one named last changes fastest.
The devices are a block of a 4x4x8 slice.
Arguments:
- tokens: bfloat16 [32, 8192, 768], P(('dp', 'ep_b', 'ep_a'))
- expert_ids: int32 [32, 8192], P(('dp', 'ep_b', 'ep_a'))
- route_order: int32 [32, 8192], P(('dp', 'ep_b', 'ep_a'))
- w_route: bfloat16 [768, 256], replicated
- expert_keys: bfloat16 [32, 256], replicated
- temperature: float32 [], replicated
- w_in: bfloat16 [32, 768, 3072], P(('ep_b', 'ep_a'))
- b_in: bfloat16 [32, 3072], P(('ep_b', 'ep_a'))
- w_out: bfloat16 [32, 3072, 768], P(('ep_b', 'ep_a'))
- b_out: bfloat16 [32, 768], P(('ep_b', 'ep_a'))
Outputs:
- output: bfloat16 [32, 8192, 768], P(('dp', 'ep_b', 'ep_a'))
All inputs are finite; a program needn't handle non-finite values.
Results may differ from a plain program's by a relative error of at most 0.00481443.
Values are sent between devices in bfloat16 or wider.
A program may use at most 768 MiB of HBM per device.

v0:
```python
import jax
import jax.numpy as jnp
from jax import lax
from jax.sharding import PartitionSpec as P

EXPERT_AXES = ("ep_b", "ep_a")


def route_local(tok_rows, id_row, order_row, w_route, expert_keys, value_a11, capacity):
    num_experts = expert_keys.shape[0]
    tok_dev = tok_rows.shape[0]
    keys_f32 = expert_keys.astype(jnp.float32)
    key_unit = keys_f32 / jnp.sqrt(jnp.sum(keys_f32 * keys_f32, axis=1, keepdims=True))
    projected = jnp.dot(tok_rows, w_route, preferred_element_type=jnp.float32)
    proj_unit = projected / jnp.sqrt(jnp.sum(projected * projected, axis=1, keepdims=True))
    router_prob = jax.nn.softmax(jnp.dot(proj_unit, key_unit.T) / value_a11, axis=1)
    expert_range = jnp.arange(num_experts, dtype=jnp.int32)[None, :]
    gate_prob = jnp.sum(jnp.where(id_row[:, None] == expert_range, router_prob, 0.0), axis=1)
    ranked_ids = jnp.take(id_row, order_row)
    ranked_hot = (ranked_ids[:, None] == expert_range).astype(jnp.int32)
    ranked_pos = jnp.sum(jnp.cumsum(ranked_hot, axis=0) * ranked_hot, axis=1) - 1
    ranked_slot = jnp.where(ranked_pos < capacity, ranked_ids * capacity + ranked_pos, num_experts * capacity)
    slot_source = jnp.full((num_experts * capacity,), tok_dev, jnp.int32).at[ranked_slot].set(order_row, mode="drop")
    dest_slot = jnp.zeros((tok_dev,), jnp.int32).at[order_row].set(ranked_slot)
    send_rows = jnp.take(tok_rows, slot_source, axis=0, mode="fill", fill_value=0)
    return send_rows, gate_prob, dest_slot


def expert_local(slot_rows, w_first, b_first, w_second, b_second):
    hidden = jnp.dot(slot_rows, w_first, preferred_element_type=jnp.float32) + b_first.astype(jnp.float32)
    hidden = jax.nn.gelu(hidden, approximate=False).astype(jnp.bfloat16)
    result = jnp.dot(hidden, w_second, preferred_element_type=jnp.float32) + b_second.astype(jnp.float32)
    return result.astype(jnp.bfloat16)


def combine_local(back_rows, dest_slot, gate_prob):
    picked = jnp.take(back_rows, dest_slot, axis=0, mode="fill", fill_value=0)
    return (gate_prob[:, None] * picked.astype(jnp.float32)).astype(jnp.bfloat16)


def solution(mesh):
    num_experts = mesh.shape["ep_b"] * mesh.shape["ep_a"]
    tok_spec = P(("dp",) + EXPERT_AXES)
    expert_spec = P(EXPERT_AXES)

    def device_step(tokens, expert_ids, route_order, w_route, expert_keys, value_a11, w_in, b_in, w_out, b_out):
        tok_dev, model_width = tokens.shape[1], tokens.shape[2]
        capacity = (5 * tok_dev + 4 * num_experts - 1) // (4 * num_experts)
        send_rows, gate_prob, dest_slot = route_local(tokens[0], expert_ids[0], route_order[0], w_route, expert_keys, value_a11, capacity)
        arrived = lax.all_to_all(send_rows.reshape(num_experts, capacity, model_width), EXPERT_AXES, 0, 0, tiled=True)
        expert_rows = expert_local(arrived.reshape(num_experts * capacity, model_width), w_in[0], b_in[0], w_out[0], b_out[0])
        returned = lax.all_to_all(expert_rows.reshape(num_experts, capacity, model_width), EXPERT_AXES, 0, 0, tiled=True)
        return combine_local(returned.reshape(num_experts * capacity, model_width), dest_slot, gate_prob)[None]

    return jax.shard_map(
        device_step,
        mesh=mesh,
        in_specs=(tok_spec, tok_spec, tok_spec, P(), P(), P(), expert_spec, expert_spec, expert_spec, expert_spec),
        out_specs=tok_spec,
        check_vma=False,
    )
```

profile of v0, /device:TPU:107, one launch (start us, length us, event | category | flops | bytes accessed | tf_op | source)
XLA Modules:
  0.0 1006.3 jit_solution(15384898130146732578)
XLA Ops:
  0.0 0.8 compare_select_fusion.1
  1.5 37.4 %gather_fusion = s32[8192]{0:T(1024)S(1)} fusion(s32[8192]{0:T(1024)} %bitcast.58, s32[8192]{0:T(1024)S(1)} %broadcast_clamp_fusion), kind=kCustom, calls=%fused_computation | custom fusion | bytes 98304 | tf_op jit(solution)/shard_map/jit(_take)/gather | solution.py:19
  38.8 0.8 bitcast_select_fusion.1
  39.7 9.5 reduce-window.6
  49.2 0.9 slice_reduce_fusion
  50.7 0.8 and_select_fusion.1
  51.5 0.8 fusion.17
  52.3 0.6 add_select_fusion
  52.9 0.9 compare_select_fusion
  53.8 30.7 %scatter_custom_fusion.1 = s32[10240]{0:T(1024)S(1)} fusion(s32[8192]{0:T(1024)S(1)} %bitcast.72, s32[8192]{0:T(1024)} %bitcast.66, s32[]{:T(128)} %constant.43.clone.1), kind=kCustom, calls=%fused_computation.65 | custom fusion | bytes 41472 | tf_op jit(solution)/shard_map/scatter | solution.py:23
  84.6 52.3 %gather_fusion.1 = bf16[10240,768]{1,0:T(8,128)(2,1)} fusion(bf16[8192,768]{1,0:T(8,128)(2,1)} %bitcast.60, s32[10240]{0:T(1024)S(1)} %fusion.20), kind=kCustom, calls=%fused_computation.1 | custom fusion | bytes 31498240 | tf_op jit(solution)/shard_map/jit(_take)/gather | solution.py:25
  136.9 13.8 %broadcast_select_fusion = bf16[32,320,768]{2,1,0:T(8,128)(2,1)} fusion(bf16[32,320,768]{2,1,0:T(8,128)(2,1)} %bitcast.61, pred[32,320]{1,0:T(8,128)(4,1)S(1)} %broadcast_in_dim.69), kind=kLoop, calls=%fused_computation.27 | loop fusion | flops 7864320 | bytes 31467520 | tf_op jit(solution)/shard_map/jit(_take)/select_n | solution.py:25
  150.7 7.7 all-to-all-start
  158.4 0.6 convert_reduce_fusion
  159.0 209.5 %all-to-all-done = bf16[32,320,768]{2,1,0:T(8,128)(2,1)} async-done(((bf16[32,320,768]{2,1,0:T(8,128)(2,1)}), bf16[32,320,768]{2,1,0:T(8,128)(2,1)}, u32[]{:S(2)}, u32[]{:S(2)}) %all-to-all-start) | async-done | bytes 15728672 | tf_op jit(solution)/shard_map/all_to_all | solution.py:50
  368.5 312.2 %fusion.2.clone.6 = bf16[10240,3072]{1,0:T(8,128)(2,1)} fusion(bf16[10240,768]{1,0:T(8,128)(2,1)} %bitcast.12, f32[3072]{0:T(1024)S(1)} %bitcast.73, bf16[1,768,3072]{2,1,0:T(8,128)(2,1)} %param.16), kind=kOutput, calls=%fused_computation.8.clone.clone.clone.clone.clone.1 | convolution fusion | flops 50394562560 | bytes 83374080 | tf_op jit(solution)/shard_map/dot_general | solution.py:30
  680.7 54.8 %add_convert_fusion = bf16[10240,768]{1,0:T(8,128)(2,1)} fusion(f32[768]{0:T(1024)S(1)} %copy-done.5, bf16[1,3072,768]{2,1,0:T(8,128)(2,1)S(1)} %copy-done.7, bf16[10240,3072]{1,0:T(8,128)(2,1)} %fusion.2.clone.6), kind=kOutput, calls=%fused_computation.24 | convolution fusion | flops 48334110720 | bytes 83364864 | tf_op jit(solution)/shard_map/dot_general | solution.py:32
  735.6 4.2 all-to-all-start.1
  739.8 30.6 %scatter_custom_fusion = s32[8192]{0:T(1024)S(1)} fusion(s32[8192]{0:T(1024)} %bitcast.69, s32[8192]{0:T(1024)} %get-tuple-element.5, s32[]{:T(128)} %constant.42.clone.1), kind=kCustom, calls=%fused_computation.69 | custom fusion | bytes 33280 | tf_op jit(solution)/shard_map/scatter | solution.py:24
  770.4 15.3 %multiply_reduce_fusion = (f32[8192]{0:T(1024)S(1)}, f32[8192,256]{0,1:T(8,128)}) fusion(bf16[768,256]{1,0:T(8,128)(2,1)S(1)} %copy-done, bf16[1,8192,768]{2,1,0:T(8,128)(2,1)} %param.10), kind=kOutput, calls=%fused_computation.30 | convolution fusion | flops 3225411584 | bytes 21397504 | tf_op jit(solution)/shard_map/dot_general | solution.py:14
  786.5 4.4 fusion.60
  791.5 157.6 %all-to-all-done.1 = bf16[32,320,768]{2,1,0:T(8,128)(2,1)} async-done(((bf16[32,320,768]{2,1,0:T(8,128)(2,1)}), bf16[32,320,768]{2,1,0:T(8,128)(2,1)}, u32[]{:S(2)}, u32[]{:S(2)}) %all-to-all-start.1) | async-done | bytes 15728672 | tf_op jit(solution)/shard_map/all_to_all | solution.py:52
  949.1 44.5 %gather_fusion.2 = bf16[8192,768]{1,0:T(8,128)(2,1)} fusion(bf16[10240,768]{1,0:T(8,128)(2,1)} %bitcast.17, s32[8192]{0:T(1024)S(1)} %fusion.22), kind=kCustom, calls=%fused_computation.2 | custom fusion | bytes 25198592 | tf_op jit(solution)/shard_map/jit(_take)/gather | solution.py:37
  993.7 12.7 %multiply_convert_fusion = bf16[1,8192,768]{2,1,0:T(8,128)(2,1)} fusion(bf16[8192,768]{1,0:T(8,128)(2,1)} %gather_fusion.2, f32[8192]{0:T(1024)S(1)} %select_reduce_fusion, pred[8192]{0:T(1024)(128)(4,1)S(1)} %compare_and_fusion.1), kind=kLoop, calls=%fused_computation.25 | loop fusion | flops 25165824 | bytes 25206784 | tf_op jit(solution)/shard_map/convert_element_type | solution.py:38
  (31 shorter events, 2.1 us)
Async XLA Ops:
  0.0 770.4 %copy-start = (bf16[768,256]{1,0:T(8,128)(2,1)S(1)}, bf16[768,256]{1,0:T(8,128)(2,1)}, u32[]{:S(2)}) copy-start(bf16[768,256]{1,0:T(8,128)(2,1)} %param.13) | copy-start | bytes 1179652
  0.8 0.6 copy-start.2
  136.9 21.5 %copy-start.4 = (bf16[1,3072]{1,0:T(2,128)(2,1)S(1)}, bf16[1,3072]{1,0:T(2,128)(2,1)}, u32[]{:S(2)}) copy-start(bf16[1,3072]{1,0:T(2,128)(2,1)} %param.17) | copy-start | bytes 18436
  136.9 21.5 %copy-start.6 = (bf16[1,768]{1,0:T(2,128)(2,1)S(1)}, bf16[1,768]{1,0:T(2,128)(2,1)}, u32[]{:S(2)}) copy-start(bf16[1,768]{1,0:T(2,128)(2,1)} %param.19) | copy-start | bytes 4612
  150.7 217.8 %all-to-all-start = ((bf16[32,320,768]{2,1,0:T(8,128)(2,1)}), bf16[32,320,768]{2,1,0:T(8,128)(2,1)}, u32[]{:S(2)}, u32[]{:S(2)}) async-start(bf16[32,320,768]{2,1,0:T(8,128)(2,1)} %broadcast_select_fusion), calls=%async_computation | async-start | bytes 31457280 | tf_op jit(solution)/shard_map/all_to_all | solution.py:50
  368.5 312.2 %copy-start.5 = (f32[768]{0:T(1024)S(1)}, f32[768]{0:T(1024)}, u32[]{:S(2)}) copy-start(f32[768]{0:T(1024)} %convert_reduce_fusion) | copy-start | bytes 9220
  368.5 312.2 %copy-start.7 = (bf16[1,3072,768]{2,1,0:T(8,128)(2,1)S(1)}, bf16[1,3072,768]{2,1,0:T(8,128)(2,1)}, u32[]{:S(2)}) copy-start(bf16[1,3072,768]{2,1,0:T(8,128)(2,1)} %param.18) | copy-start | bytes 14155780
  680.7 105.0 %copy-start.3 = (bf16[32,256]{1,0:T(8,128)(2,1)S(1)}, bf16[32,256]{1,0:T(8,128)(2,1)}, u32[]{:S(2)}) copy-start(bf16[32,256]{1,0:T(8,128)(2,1)} %param.14) | copy-start | bytes 49156
  735.6 55.6 %copy-start.1 = (s32[1,8192]{1,0:T(1,128)S(1)}, s32[1,8192]{1,0:T(1,128)}, u32[]{:S(2)}) copy-start(s32[1,8192]{1,0:T(1,128)} %param.11) | copy-start | bytes 98308
  735.6 213.6 %all-to-all-start.1 = ((bf16[32,320,768]{2,1,0:T(8,128)(2,1)}), bf16[32,320,768]{2,1,0:T(8,128)(2,1)}, u32[]{:S(2)}, u32[]{:S(2)}) async-start(bf16[32,320,768]{2,1,0:T(8,128)(2,1)} %bitcast.62), calls=%async_computation.1 | async-start | bytes 31457280 | tf_op jit(solution)/shard_map/all_to_all | solution.py:52
where the time goes:
time: 1010 us
  matrix products  387 us (38%)
  waiting for transfers between devices  367 us (36%)
  local copies, waits for them, and re-layouts  197 us (20%)
  other arithmetic  42.7 us (4%)
  starting transfers between devices  11.9 us (1%)
    dot_general x1, matrix products, expert_local(): jnp.dot(slot_rows, w_first, preferred_element_type=jnp.float32)  312 us
    all_to_all x1, waiting for transfers between devices, device_step(): lax.all_to_all(send_rows.reshape(num_experts, capacity, model_width), EXP...  210 us
    all_to_all x1, waiting for transfers between devices, device_step(): lax.all_to_all(expert_rows.reshape(num_experts, capacity, model_width), E...  158 us
    dot_general x1, matrix products, expert_local(): jnp.dot(hidden, w_second, preferred_element_type=jnp.float32)  54.8 us
    gather x1, local copies, waits for them, and re-layouts, route_local(): jnp.take(tok_rows, slot_source, axis=0, mode='fill', fill_value=0)  52.3 us
    gather x1, local copies, waits for them, and re-layouts, combine_local(): picked = jnp.take(back_rows, dest_slot, axis=0, mode='fill', fill_value=0)  44.5 us
    gather x1, local copies, waits for them, and re-layouts, route_local(): ranked_ids = jnp.take(id_row, order_row)  37.4 us
    scatter x1, local copies, waits for them, and re-layouts, route_local(): jnp.full((num_experts * capacity,), tok_dev, jnp.int32).at[ranked_slot]  30.7 us
  transfers between devices with their start and end apart: 2, of which 2 were waited for; matrix products, arithmetic and copies ran while one was open for 5% of the time, Pallas kernels for 0%

commit v1 on v0

v1 whole, which is shorter than its diff:
```python
import functools

import jax
import jax.numpy as jnp
from jax import lax
from jax.experimental import pallas as pl
from jax.experimental.pallas import tpu as pltpu
from jax.sharding import PartitionSpec as P

EXPERT_AXES = ("ep_b", "ep_a")
MESH = pl.DeviceIdType.MESH
LANES = 128


def hot(values, size):
    return (values[:, None] == jnp.arange(size, dtype=jnp.int32)[None, :]).astype(jnp.bfloat16)


def bdot(a, b):
    return jnp.dot(a, b, preferred_element_type=jnp.float32)


def route_slots(id_row, order_row, num_experts, capacity):
    tok_dev = id_row.shape[0]
    rows = tok_dev // LANES
    slots = num_experts * capacity
    order_hi, order_lo = order_row // LANES, order_row % LANES
    hot_hi, hot_lo = hot(order_hi, rows), hot(order_lo, LANES)
    id_table = id_row.reshape(rows, LANES).astype(jnp.bfloat16)
    ranked_ids = jnp.sum(bdot(hot_hi, id_table) * hot_lo.astype(jnp.float32), axis=1).astype(jnp.int32)
    ranked_hot = hot(ranked_ids, num_experts)
    span = 256
    blocks = ranked_hot.reshape(tok_dev // span, span, num_experts)
    lower = (jnp.arange(span)[:, None] >= jnp.arange(span)[None, :]).astype(jnp.bfloat16)
    within = jnp.einsum("ij,bje->bie", lower, blocks, preferred_element_type=jnp.float32)
    totals = within[:, -1, :]
    before = jnp.cumsum(totals, axis=0) - totals
    ranked_pos = jnp.sum((within + before[:, None, :]) * blocks.astype(jnp.float32), axis=2).reshape(tok_dev)
    ranked_pos = ranked_pos.astype(jnp.int32) - 1
    ranked_slot = jnp.where(ranked_pos < capacity, ranked_ids * capacity + ranked_pos, slots)
    slot_hi, slot_lo = ranked_slot // LANES, ranked_slot % LANES
    as_col = lambda v: v.astype(jnp.bfloat16)[:, None]
    dims = (((0,), (0,)), ((), ()))
    pair = jnp.concatenate([as_col(slot_hi) * hot_lo, as_col(slot_lo) * hot_lo], axis=1)
    table = lax.dot_general(hot_hi, pair, dims, preferred_element_type=jnp.float32).astype(jnp.int32)
    dest_slot = (table[:, :LANES] * LANES + table[:, LANES:]).reshape(tok_dev)
    shot_hi, shot_lo = hot(slot_hi, slots // LANES), hot(slot_lo, LANES)
    pair = jnp.concatenate([as_col(order_hi) * shot_lo, as_col(order_lo) * shot_lo], axis=1)
    table = lax.dot_general(shot_hi, pair, dims, preferred_element_type=jnp.float32).astype(jnp.int32)
    slot_source = (table[:, :LANES] * LANES + table[:, LANES:]).reshape(slots)
    return slot_source, dest_slot


def gates(tok_rows, id_row, w_route, expert_keys, tau):
    num_experts = expert_keys.shape[0]
    keys_f32 = expert_keys.astype(jnp.float32)
    key_unit = keys_f32 / jnp.sqrt(jnp.sum(keys_f32 * keys_f32, axis=1, keepdims=True))
    projected = jnp.dot(tok_rows, w_route, preferred_element_type=jnp.float32)
    proj_unit = projected / jnp.sqrt(jnp.sum(projected * projected, axis=1, keepdims=True))
    router_prob = jax.nn.softmax(jnp.dot(proj_unit, key_unit.T) / tau, axis=1)
    expert_range = jnp.arange(num_experts, dtype=jnp.int32)[None, :]
    return jnp.sum(jnp.where(id_row[:, None] == expert_range, router_prob, 0.0), axis=1)


def send_order(nb, nx):
    rest = [(y, x) for y in range(nb) for x in range(nx) if (y, x) != (0, 0)]

    def phase(off):
        y, x = off
        near = lambda v, n: v in (1, n - 1)
        if x == 0 or y == 0:
            return 0 if near(x, nx) or near(y, nb) else 3
        if near(x, nx) and near(y, nb):
            return 1 if (x == 1) == (y == 1) else 2
        return 4 if not near(x, nx) and not near(y, nb) else 5

    rest.sort(key=phase)
    out = [(0, 0, 0), (0, 0, 1)]
    for p in range(6):
        out += [(y, x, c) for c in range(2) for (y, x) in rest if phase((y, x)) == p]
    return out


def exchange_kernel(order, nb, nx, s_ref, w1_hbm, b1_ref, w2_hbm, b2_ref, r_ref,
                    a_buf, h_buf, w1_v, w2_v, wsem, lsem, send1, recv1, send2, recv2):
    count = len(order)
    row_b, row_a = lax.axis_index("ep_b"), lax.axis_index("ep_a")
    row_x, row_c = row_a // 2, lax.rem(row_a, 2)
    me = row_b * (2 * nx) + row_a
    w1_copy = pltpu.make_async_copy(w1_hbm, w1_v, wsem.at[0])
    w2_copy = pltpu.make_async_copy(w2_hbm, w2_v, wsem.at[1])
    own_in = pltpu.make_async_copy(s_ref.at[me], a_buf.at[0], lsem.at[0])
    w1_copy.start()
    w2_copy.start()
    own_in.start()

    def peer(y, x, c):
        return lax.rem(row_b + y, nb), lax.rem(row_x + x, nx) * 2 + lax.rem(row_c + c, 2)

    barrier = pltpu.get_barrier_semaphore()
    for y, x, c in order[1:]:
        pb, pa = peer(y, x, c)
        pl.semaphore_signal(barrier, inc=1, device_id={"ep_b": pb, "ep_a": pa}, device_id_type=MESH)
    pl.semaphore_wait(barrier, count - 1)

    out_copies = []
    for k in range(1, count):
        pb, pa = peer(*order[k])
        copy = pltpu.make_async_remote_copy(
            src_ref=s_ref.at[pb * (2 * nx) + pa], dst_ref=a_buf.at[k], send_sem=send1.at[k], recv_sem=recv1.at[k],
            device_id={"ep_b": pb, "ep_a": pa}, device_id_type=MESH)
        copy.start()
        out_copies.append(copy)

    words = []
    for w in range(0, count, 5):
        word = 0
        for j, (y, x, c) in enumerate(order[w:w + 5]):
            word += (((-y) % nb) * (2 * nx) + ((-x) % nx) * 2 + c) << (6 * j)
        words.append(word)

    def back_copy(k):
        word = 0
        for w, value in enumerate(words):
            word = word + jnp.where(k // 5 == w, value, 0)
        code = lax.rem(lax.shift_right_logical(word, 6 * lax.rem(k, 5)), 64)
        pb, pa = peer(code // (2 * nx), lax.rem(code // 2, nx), lax.rem(code, 2))
        return pltpu.make_async_remote_copy(
            src_ref=a_buf.at[k], dst_ref=r_ref.at[me], send_sem=send2.at[k], recv_sem=recv2.at[k],
            device_id={"ep_b": pb, "ep_a": pa}, device_id_type=MESH)

    rows = 2 * a_buf.shape[1]
    hidden, width = w1_v.shape[1], w1_v.shape[0]
    n1, n2 = 512, 256

    def mlp(pair):
        x = a_buf[pl.ds(pair * 2, 2)].reshape(rows, width)
        for n in range(0, hidden, n1):
            part = jnp.dot(x, w1_v[:, n:n + n1], preferred_element_type=jnp.float32) + b1_ref[:, n:n + n1]
            part = 0.5 * part * (1.0 + lax.erf(part * 0.7071067811865476))
            h_buf[:, n:n + n1] = part.astype(jnp.bfloat16)
        for n in range(0, width, n2):
            y = jnp.dot(h_buf[...], w2_v[:, n:n + n2], preferred_element_type=jnp.float32) + b2_ref[:, n:n + n2]
            a_buf[pl.ds(pair * 2, 2), :, n:n + n2] = y.astype(jnp.bfloat16).reshape(2, rows // 2, n2)

    own_in.wait()
    w1_copy.wait()
    w2_copy.wait()
    out_copies[0].wait_recv()
    mlp(0)
    own_out = pltpu.make_async_copy(a_buf.at[0], r_ref.at[me], lsem.at[1])
    own_out.start()
    back_copy(1).start()

    near_b, near_a = peer(*order[1])

    def arrived(k):
        pltpu.make_async_remote_copy(
            src_ref=s_ref.at[me], dst_ref=a_buf.at[k], send_sem=send1.at[k], recv_sem=recv1.at[k],
            device_id={"ep_b": near_b, "ep_a": near_a}, device_id_type=MESH).wait_recv()

    def loop_step(pair, carry):
        arrived(2 * pair)
        arrived(2 * pair + 1)
        mlp(pair)
        back_copy(2 * pair).start()
        back_copy(2 * pair + 1).start()
        return carry

    lax.fori_loop(1, count // 2, loop_step, 0)
    own_out.wait()
    for copy in out_copies:
        copy.wait_send()

    def drain(k, carry):
        copy = back_copy(k)
        copy.wait_send()
        copy.wait_recv()
        return carry

    lax.fori_loop(1, count, drain, 0)


def exchange(send_rows, w_first, b_first, w_second, b_second, nb, na):
    count, capacity, width = send_rows.shape
    hidden = w_first.shape[1]
    nx = na // 2
    order = send_order(nb, nx)
    any_spec = pl.BlockSpec(memory_space=pl.ANY)
    vmem_spec = pl.BlockSpec(memory_space=pltpu.VMEM)
    flops = 4 * count * capacity * width * hidden
    return pl.pallas_call(
        functools.partial(exchange_kernel, order, nb, nx),
        name="exchange_mlp",
        out_shape=jax.ShapeDtypeStruct((count, capacity, width), jnp.bfloat16),
        in_specs=[any_spec, any_spec, vmem_spec, any_spec, vmem_spec],
        out_specs=any_spec,
        scratch_shapes=[
            pltpu.VMEM((count, capacity, width), jnp.bfloat16),
            pltpu.VMEM((2 * capacity, hidden), jnp.bfloat16),
            pltpu.VMEM((width, hidden), jnp.bfloat16),
            pltpu.VMEM((hidden, width), jnp.bfloat16),
            pltpu.SemaphoreType.DMA((2,)),
            pltpu.SemaphoreType.DMA((2,)),
            pltpu.SemaphoreType.DMA((count,)),
            pltpu.SemaphoreType.DMA((count,)),
            pltpu.SemaphoreType.DMA((count,)),
            pltpu.SemaphoreType.DMA((count,)),
        ],
        cost_estimate=pl.CostEstimate(flops=flops, bytes_accessed=4 * count * capacity * width, transcendentals=0),
        compiler_params=pltpu.CompilerParams(
            collective_id=0, has_side_effects=True, vmem_limit_bytes=60 * 1024 * 1024),
    )(send_rows, w_first, b_first.astype(jnp.float32)[None], w_second, b_second.astype(jnp.float32)[None])


def combine_local(back_rows, dest_slot, gate_prob):
    picked = jnp.take(back_rows, dest_slot, axis=0, mode="fill", fill_value=0)
    return (gate_prob[:, None] * picked.astype(jnp.float32)).astype(jnp.bfloat16)


def solution(mesh):
    nb, na = mesh.shape["ep_b"], mesh.shape["ep_a"]
    num_experts = nb * na
    tok_spec = P(("dp",) + EXPERT_AXES)
    expert_spec = P(EXPERT_AXES)

    def device_step(tokens, expert_ids, route_order, w_route, expert_keys, tau, w_in, b_in, w_out, b_out):
        tok_dev, model_width = tokens.shape[1], tokens.shape[2]
        capacity = (5 * tok_dev + 4 * num_experts - 1) // (4 * num_experts)
        slot_source, dest_slot = route_slots(expert_ids[0], route_order[0], num_experts, capacity)
        send_rows = jnp.take(tokens[0], slot_source, axis=0, mode="clip").reshape(num_experts, capacity, model_width)
        gate_prob = gates(tokens[0], expert_ids[0], w_route, expert_keys, tau)
        returned = exchange(send_rows, w_in[0], b_in[0], w_out[0], b_out[0], nb, na)
        return combine_local(returned.reshape(num_experts * capacity, model_width), dest_slot, gate_prob)[None]

    return jax.shard_map(
        device_step,
        mesh=mesh,
        in_specs=(tok_spec, tok_spec, tok_spec, P(), P(), P(), expert_spec, expert_spec, expert_spec, expert_spec),
        out_specs=tok_spec,
        check_vma=False,
    )
```

time: 1010 us -> 551 us (0.55)
  the two profiles are of different devices: /device:TPU:107 before, /device:TPU:120 now
where the time goes in v1:
time: 551 us
  Pallas kernels  417 us (76%)
  local copies, waits for them, and re-layouts  97.7 us (18%)
  other arithmetic  22.7 us (4%)
  matrix products  12.5 us (2%)
    pallas_call x1, Pallas kernels, exchange(): pl.pallas_call(functools.partial(exchange_kernel, order, nb, nx), name='e...  417 us
    gather x1, local copies, waits for them, and re-layouts, device_step(): jnp.take(tokens[0], slot_source, axis=0, mode='clip')  52.3 us
    gather x1, local copies, waits for them, and re-layouts, combine_local(): picked = jnp.take(back_rows, dest_slot, axis=0, mode='fill', fill_value=0)  44.5 us
    convert_element_type x1, other arithmetic, combine_local(): (gate_prob[:, None] * picked.astype(jnp.float32)).astype(jnp.bfloat16)  12.7 us

profile of v1, /device:TPU:120, one launch (start us, length us, event | category | flops | bytes accessed | tf_op | source)
XLA Modules:
  0.0 550.6 jit_solution(13315537413925440069)
XLA Ops:
  0.7 0.8 fusion.32
  1.5 1.3 convert_element_type.144.b2_ref
  2.8 1.3 convert_element_type.143.b1_ref
  4.2 0.8 convert_reduce_fusion
  5.0 0.8 fusion.45
  5.8 1.3 fusion.15
  7.1 0.4 convolution_bitcast_fusion
  7.7 0.3 copy.17
  8.0 0.3 copy.18
  8.3 0.4 subtract_reduce_fusion
  8.7 0.4 multiply_reduce_fusion.1
  9.1 1.7 fusion.10
  10.8 1.4 fusion.17
  12.2 1.4 fusion.20
  13.6 0.6 compare_and_fusion
  14.3 0.6 broadcast_clamp_fusion
  14.9 6.9 %multiply_reduce_fusion = (f32[8192]{0:T(1024)S(1)}, f32[8192,256]{0,1:T(8,128)S(1)}) fusion(bf16[768,256]{1,0:T(8,128)(2,1)S(1)} %copy-done, bf16[1,8192,768]{2,1,0:T(8,128)(2,1)} %param.10), kind=kOutput, calls=%fused_computation.6 | convolution fusion | flops 3225411584 | bytes 21397504 | tf_op jit(solution)/shard_map/dot_general | solution.py:58
  21.9 1.2 fusion.47
  23.0 0.2 fusion.26
  23.3 0.9 select_reduce_fusion
  24.2 52.3 %gather_fusion = bf16[10240,768]{1,0:T(8,128)(2,1)} fusion(bf16[8192,768]{1,0:T(8,128)(2,1)} %bitcast.38, s32[10240]{0:T(1024)S(1)} %fusion.31), kind=kCustom, calls=%fused_computation | custom fusion | bytes 31498240 | tf_op jit(solution)/shard_map/jit(_take)/gather | solution.py:231
  76.5 416.8 %exchange_mlp.1 = bf16[32,320,768]{2,1,0:T(8,128)(2,1)} custom-call(bf16[32,320,768]{2,1,0:T(8,128)(2,1)} %bitcast.40, bf16[768,3072]{1,0:T(8,128)(2,1)} %bitcast.46, f32[1,3072]{1,0:T(1,128)} %convert_element_type.143.b1_ref, bf16[3072,768]{1,0:T(8,128)(2,1)} %bitcast.47, f32[1,768]{1,0:T(1,128)} %convert_element_type.144.b2_ref), custom_call_target="tpu_custom_call" | custom-call | flops 96636764160 | bytes 31457280 | tf_op jit(solution)/shard_map/exchange_mlp/pallas_call | solution.py:192
  493.3 44.5 %gather_fusion.1 = bf16[8192,768]{1,0:T(8,128)(2,1)} fusion(bf16[10240,768]{1,0:T(8,128)(2,1)} %bitcast.39, s32[8192]{0:T(1024)S(1)} %copy-done.4), kind=kCustom, calls=%fused_computation.1 | custom fusion | bytes 25198592 | tf_op jit(solution)/shard_map/jit(_take)/gather | solution.py:217
  537.9 12.7 %multiply_convert_fusion = bf16[1,8192,768]{2,1,0:T(8,128)(2,1)} fusion(bf16[8192,768]{1,0:T(8,128)(2,1)} %gather_fusion.1, f32[8192]{0:T(1024)S(1)} %copy-done.2, pred[8192]{0:T(1024)(128)(4,1)S(1)} %copy-done.5), kind=kLoop, calls=%fused_computation.2 | loop fusion | flops 25165824 | bytes 25206784 | tf_op jit(solution)/shard_map/convert_element_type | solution.py:218
  (25 shorter events, 0.4 us)
Async XLA Ops:
  0.0 14.9 %copy-start = (bf16[768,256]{1,0:T(8,128)(2,1)S(1)}, bf16[768,256]{1,0:T(8,128)(2,1)}, u32[]{:S(2)}) copy-start(bf16[768,256]{1,0:T(8,128)(2,1)} %param.13) | copy-start | bytes 1179652
  14.9 6.9 %copy-start.6 = (bf16[32,256]{1,0:T(8,128)(2,1)S(1)}, bf16[32,256]{1,0:T(8,128)(2,1)}, u32[]{:S(2)}) copy-start(bf16[32,256]{1,0:T(8,128)(2,1)} %param.14) | copy-start | bytes 49156
  21.9 1.4 copy-start.3
  76.5 416.8 %copy-start.4 = (s32[8192]{0:T(1024)S(1)}, s32[8192]{0:T(1024)}, u32[]{:S(2)}) copy-start(s32[8192]{0:T(1024)} %broadcast_clamp_fusion) | copy-start | bytes 98308
  493.3 44.6 %copy-start.2 = (f32[8192]{0:T(1024)S(1)}, f32[8192]{0:T(1024)}, u32[]{:S(2)}) copy-start(f32[8192]{0:T(1024)} %select_reduce_fusion) | copy-start | bytes 98308
  493.3 44.6 %copy-start.5 = (pred[8192]{0:T(1024)(128)(4,1)S(1)}, pred[8192]{0:T(1024)(128)(4,1)}, u32[]{:S(2)}) copy-start(pred[8192]{0:T(1024)(128)(4,1)} %get-tuple-element.5) | copy-start | bytes 24580
  537.9 12.7 %copy-start.1 = (bf16[768,256]{1,0:T(8,128)(2,1)S(1)}, bf16[768,256]{1,0:T(8,128)(2,1)}, u32[]{:S(2)}) copy-start(bf16[768,256]{1,0:T(8,128)(2,1)} %param.13) | copy-start | bytes 1179652

commit v2 on v1

v2 whole, which is shorter than its diff:
```python
import functools

import jax
import jax.numpy as jnp
from jax import lax
from jax.experimental import pallas as pl
from jax.experimental.pallas import tpu as pltpu
from jax.sharding import PartitionSpec as P

EXPERT_AXES = ("ep_b", "ep_a")
MESH = pl.DeviceIdType.MESH
LANES = 128


def hot(values, size):
    return (values[:, None] == jnp.arange(size, dtype=jnp.int32)[None, :]).astype(jnp.bfloat16)


def bdot(a, b):
    return jnp.dot(a, b, preferred_element_type=jnp.float32)


def route_slots(id_row, order_row, num_experts, capacity):
    tok_dev = id_row.shape[0]
    rows = tok_dev // LANES
    slots = num_experts * capacity
    order_hi, order_lo = order_row // LANES, order_row % LANES
    hot_hi, hot_lo = hot(order_hi, rows), hot(order_lo, LANES)
    id_table = id_row.reshape(rows, LANES).astype(jnp.bfloat16)
    ranked_ids = jnp.sum(bdot(hot_hi, id_table) * hot_lo.astype(jnp.float32), axis=1).astype(jnp.int32)
    ranked_hot = hot(ranked_ids, num_experts)
    span = 256
    blocks = ranked_hot.reshape(tok_dev // span, span, num_experts)
    lower = (jnp.arange(span)[:, None] >= jnp.arange(span)[None, :]).astype(jnp.bfloat16)
    within = jnp.einsum("ij,bje->bie", lower, blocks, preferred_element_type=jnp.float32)
    totals = within[:, -1, :]
    before = jnp.cumsum(totals, axis=0) - totals
    ranked_pos = jnp.sum((within + before[:, None, :]) * blocks.astype(jnp.float32), axis=2).reshape(tok_dev)
    ranked_pos = ranked_pos.astype(jnp.int32) - 1
    ranked_slot = jnp.where(ranked_pos < capacity, ranked_ids * capacity + ranked_pos, slots)
    slot_hi, slot_lo = ranked_slot // LANES, ranked_slot % LANES
    as_col = lambda v: v.astype(jnp.bfloat16)[:, None]
    dims = (((0,), (0,)), ((), ()))
    pair = jnp.concatenate([as_col(slot_hi) * hot_lo, as_col(slot_lo) * hot_lo], axis=1)
    table = lax.dot_general(hot_hi, pair, dims, preferred_element_type=jnp.float32).astype(jnp.int32)
    dest_slot = (table[:, :LANES] * LANES + table[:, LANES:]).reshape(tok_dev)
    shot_hi, shot_lo = hot(slot_hi, slots // LANES), hot(slot_lo, LANES)
    pair = jnp.concatenate([as_col(order_hi) * shot_lo, as_col(order_lo) * shot_lo], axis=1)
    table = lax.dot_general(shot_hi, pair, dims, preferred_element_type=jnp.float32).astype(jnp.int32)
    slot_source = (table[:, :LANES] * LANES + table[:, LANES:]).reshape(slots)
    return slot_source, dest_slot


def send_order(nb, nx):
    rest = [(y, x) for y in range(nb) for x in range(nx) if (y, x) != (0, 0)]

    def phase(off):
        y, x = off
        near = lambda v, n: v in (1, n - 1)
        if x == 0 or y == 0:
            return 0 if near(x, nx) or near(y, nb) else 3
        if near(x, nx) and near(y, nb):
            return 1 if (x == 1) == (y == 1) else 2
        return 4 if not near(x, nx) and not near(y, nb) else 5

    rest.sort(key=phase)
    out = [(0, 0, 0), (0, 0, 1)]
    for p in range(6):
        out += [(y, x, c) for c in range(2) for (y, x) in rest if phase((y, x)) == p]
    return out


def exchange_kernel(order, nb, nx, source_ref, ids_ref, tau_ref, tok_hbm, wr_ref, key_ref, w1_hbm, b1_ref, w2_hbm, b2_ref,
                    r_ref, s_ref, gate_ref, wide, a_buf, h_buf, w1_v, w2_v, gathered, stage,
                    wsem, lsem, tsem, gsem, send1, recv1, send2, recv2):
    count, capacity, width = a_buf.shape
    hidden = w1_v.shape[1]
    tok_dev = tok_hbm.shape[0]
    parts = width // LANES
    row_b, row_a = lax.axis_index("ep_b"), lax.axis_index("ep_a")
    row_x, row_c = row_a // 2, lax.rem(row_a, 2)
    me = row_b * (2 * nx) + row_a

    def peer(y, x, c):
        return lax.rem(row_b + y, nb), lax.rem(row_x + x, nx) * 2 + lax.rem(row_c + c, 2)

    barrier = pltpu.get_barrier_semaphore()
    for y, x, c in order[1:]:
        pb, pa = peer(y, x, c)
        pl.semaphore_signal(barrier, inc=1, device_id={"ep_b": pb, "ep_a": pa}, device_id_type=MESH)

    chunk, depth = 512, h_buf.shape[0]
    chunks = tok_dev // chunk

    def token_load(i):
        slot = lax.rem(i, depth)
        return pltpu.make_async_copy(
            tok_hbm.at[pl.ds(pl.multiple_of(i * chunk, chunk), chunk)], h_buf.at[slot, pl.ds(0, chunk)], tsem.at[slot])

    for i in range(depth - 1):
        token_load(i).start()

    def widen(i, carry):
        @pl.when(i + depth - 1 < chunks)
        def _():
            token_load(i + depth - 1).start()
        token_load(i).wait()
        for j in range(parts):
            piece = h_buf[lax.rem(i, depth), pl.ds(0, chunk), j * LANES:(j + 1) * LANES].astype(jnp.float32)
            wide[pl.ds(i * chunk * parts + j, chunk, stride=parts), :] = piece
        return carry

    lax.fori_loop(0, chunks, widen, 0)
    w1_copy = pltpu.make_async_copy(w1_hbm, w1_v, wsem.at[0])
    w2_copy = pltpu.make_async_copy(w2_hbm, w2_v, wsem.at[1])
    w1_copy.start()
    w2_copy.start()

    words = []
    for w in range(0, count, 5):
        word = 0
        for j, (y, x, c) in enumerate(order[w:w + 5]):
            word += (y * (2 * nx) + x * 2 + c) << (6 * j)
        words.append(word)

    def offset(k):
        word = 0
        for w, value in enumerate(words):
            word = word + jnp.where(k // 5 == w, value, 0)
        code = lax.rem(lax.shift_right_logical(word, 6 * lax.rem(k, 5)), 64)
        return code // (2 * nx), lax.rem(code // 2, nx), lax.rem(code, 2)

    def fill(block, slot):
        def rows16(r, carry):
            for q in range(16):
                src = source_ref[block * capacity + r * 16 + q]
                gathered[pl.ds((r * 16 + q) * parts, parts), :] = wide[pl.ds(src * parts, parts), :]
            return carry
        lax.fori_loop(0, capacity // 16, rows16, 0)
        for j in range(parts):
            stage[slot, :, j * LANES:(j + 1) * LANES] = gathered[pl.ds(j, capacity, stride=parts), :].astype(jnp.bfloat16)

    def stage_copy(k, slot):
        y, x, c = offset(k)
        pb, pa = peer(y, x, c)
        return pltpu.make_async_copy(stage.at[slot], s_ref.at[pb * (2 * nx) + pa], gsem.at[slot])

    def send_copy(k):
        y, x, c = offset(k)
        pb, pa = peer(y, x, c)
        return pltpu.make_async_remote_copy(
            src_ref=s_ref.at[pb * (2 * nx) + pa], dst_ref=a_buf.at[k], send_sem=send1.at[k], recv_sem=recv1.at[k],
            device_id={"ep_b": pb, "ep_a": pa}, device_id_type=MESH)

    def back_copy(k):
        y, x, c = offset(k)
        pb, pa = peer(nb - y, nx - x, c)
        return pltpu.make_async_remote_copy(
            src_ref=a_buf.at[k], dst_ref=r_ref.at[me], send_sem=send2.at[k], recv_sem=recv2.at[k],
            device_id={"ep_b": pb, "ep_a": pa}, device_id_type=MESH)

    pl.semaphore_wait(barrier, count - 1)

    def fill_step(k, carry):
        y, x, c = offset(k)
        pb, pa = peer(y, x, c)
        slot = lax.rem(k, 2)
        fill(pb * (2 * nx) + pa, slot)
        stage_copy(k, slot).start()

        @pl.when(k > 1)
        def _():
            stage_copy(k - 1, 1 - slot).wait()
            send_copy(k - 1).start()
        return carry

    lax.fori_loop(1, count, fill_step, 0)
    stage_copy(count - 1, (count - 1) % 2).wait()
    send_copy(count - 1).start()
    fill(me, 0)
    own_in = pltpu.make_async_copy(stage.at[0], s_ref.at[me], lsem.at[0])
    own_in.start()
    own_in.wait()
    own_in = pltpu.make_async_copy(s_ref.at[me], a_buf.at[0], lsem.at[0])
    own_in.start()

    rows = 2 * capacity
    n1, n2 = 384, 256
    per = width // n1

    def mlp(pair):
        x = a_buf[pl.ds(pair * 2, 2)].reshape(rows, width)
        for n in range(hidden // n1):
            cols = pl.ds(n * n1, n1)
            part = jnp.dot(x, w1_v[:, cols], preferred_element_type=jnp.float32) + b1_ref[:, cols]
            part = 0.5 * part * (1.0 + lax.erf(part * 0.7071067811865476))
            h_buf[n // per, :, (n % per) * n1:(n % per + 1) * n1] = part.astype(jnp.bfloat16)
        for n in range(0, width, n2):
            h = jnp.concatenate([h_buf[q] for q in range(depth)], axis=1)
            y = jnp.dot(h, w2_v[:, n:n + n2], preferred_element_type=jnp.float32) + b2_ref[:, n:n + n2]
            a_buf[pl.ds(pair * 2, 2), :, n:n + n2] = y.astype(jnp.bfloat16).reshape(2, capacity, n2)

    own_in.wait()
    w1_copy.wait()
    w2_copy.wait()

    def loop_step(pair, carry):
        @pl.when(pair > 0)
        def _():
            send_copy(2 * pair).wait_recv()
        send_copy(2 * pair + 1).wait_recv()
        mlp(pair)

        @pl.when(pair > 0)
        def _():
            back_copy(2 * pair).start()
        back_copy(2 * pair + 1).start()
        return carry

    lax.fori_loop(0, count // 2, loop_step, 0)
    own_out = pltpu.make_async_copy(a_buf.at[0], r_ref.at[me], lsem.at[1])
    own_out.start()

    key = key_ref[...].astype(jnp.float32)
    key_unit = key / jnp.sqrt(jnp.sum(key * key, axis=1, keepdims=True))
    for i in range(depth - 1):
        token_load(i).start()

    def gate_step(i, carry):
        @pl.when(i + depth - 1 < chunks)
        def _():
            token_load(i + depth - 1).start()
        token_load(i).wait()
        x = h_buf[lax.rem(i, depth), pl.ds(0, chunk), :]
        proj = lax.dot_general(wr_ref[...], x, (((1,), (1,)), ((), ())), preferred_element_type=jnp.float32)
        unit = proj / jnp.sqrt(jnp.sum(proj * proj, axis=0, keepdims=True))
        logits = jnp.dot(key_unit, unit, precision=lax.Precision.HIGHEST, preferred_element_type=jnp.float32) / tau_ref[0, 0]
        weight = jnp.exp(logits - jnp.max(logits, axis=0, keepdims=True))
        cols = pl.ds(pl.multiple_of(i * chunk, chunk), chunk)
        expert = lax.broadcasted_iota(jnp.int32, weight.shape, 0)
        mine = jnp.sum(jnp.where(expert == ids_ref[:, cols], weight, 0.0), axis=0, keepdims=True)
        gate_ref[:, cols] = mine / jnp.sum(weight, axis=0, keepdims=True)
        return carry

    lax.fori_loop(0, chunks, gate_step, 0)
    own_out.wait()

    def drain(k, carry):
        send_copy(k).wait_send()
        copy = back_copy(k)
        copy.wait_send()
        copy.wait_recv()
        return carry

    lax.fori_loop(1, count, drain, 0)


def exchange(tokens, id_row, slot_source, w_route, expert_keys, tau, w_first, b_first, w_second, b_second, nb, na):
    tok_dev, width = tokens.shape
    count = nb * na
    capacity = slot_source.shape[0] // count
    hidden = w_first.shape[1]
    nx = na // 2
    order = send_order(nb, nx)
    any_spec = pl.BlockSpec(memory_space=pl.ANY)
    vmem_spec = pl.BlockSpec(memory_space=pltpu.VMEM)
    smem_spec = pl.BlockSpec(memory_space=pltpu.SMEM)
    flops = 4 * count * capacity * width * hidden
    blocks = jax.ShapeDtypeStruct((count, capacity, width), jnp.bfloat16)
    dma = lambda n: pltpu.SemaphoreType.DMA((n,))
    returned, _, gate = pl.pallas_call(
        functools.partial(exchange_kernel, order, nb, nx),
        name="exchange_mlp",
        out_shape=(blocks, blocks, jax.ShapeDtypeStruct((1, tok_dev), jnp.float32)),
        in_specs=[smem_spec, vmem_spec, smem_spec, any_spec, vmem_spec, vmem_spec, any_spec, vmem_spec, any_spec, vmem_spec],
        out_specs=(any_spec, any_spec, vmem_spec),
        scratch_shapes=[
            pltpu.VMEM((tok_dev * (width // LANES), LANES), jnp.float32),
            pltpu.VMEM((count, capacity, width), jnp.bfloat16),
            pltpu.VMEM((hidden // width, 2 * capacity, width), jnp.bfloat16),
            pltpu.VMEM((width, hidden), jnp.bfloat16),
            pltpu.VMEM((hidden, width), jnp.bfloat16),
            pltpu.VMEM((capacity * (width // LANES), LANES), jnp.float32),
            pltpu.VMEM((2, capacity, width), jnp.bfloat16),
            dma(2), dma(2), dma(hidden // width), dma(2), dma(count), dma(count), dma(count), dma(count),
        ],
        cost_estimate=pl.CostEstimate(flops=flops, bytes_accessed=6 * count * capacity * width, transcendentals=0),
        compiler_params=pltpu.CompilerParams(
            collective_id=0, has_side_effects=True, vmem_limit_bytes=67000000),
    )(slot_source, id_row[None], tau.reshape(1, 1), tokens, w_route.T, expert_keys,
      w_first, b_first.astype(jnp.float32)[None], w_second, b_second.astype(jnp.float32)[None])
    return returned.reshape(count * capacity, width), gate.reshape(tok_dev)


def combine_kernel(dest_ref, gate_ref, back_ref, out_ref, wide, gathered, in_buf, out_buf, in_sem, out_sem):
    slots, width = back_ref.shape
    tokens = out_ref.shape[0]
    parts = width // LANES
    rows = in_buf.shape[1]
    depth = in_buf.shape[0]
    loads = slots // rows

    def load(i):
        return pltpu.make_async_copy(back_ref.at[pl.ds(pl.multiple_of(i * rows, rows), rows)], in_buf.at[lax.rem(i, depth)], in_sem.at[lax.rem(i, depth)])

    for i in range(depth - 1):
        load(i).start()
    wide[pl.ds(slots * parts, 8), :] = jnp.zeros((8, LANES), jnp.float32)

    def widen(i, carry):
        @pl.when(i + depth - 1 < loads)
        def _():
            load(i + depth - 1).start()
        load(i).wait()
        for j in range(parts):
            piece = in_buf[lax.rem(i, depth), :, j * LANES:(j + 1) * LANES].astype(jnp.float32)
            wide[pl.ds(i * rows * parts + j, rows, stride=parts), :] = piece
        return carry

    lax.fori_loop(0, loads, widen, 0)

    def store(i):
        return pltpu.make_async_copy(out_buf.at[lax.rem(i, 2)], out_ref.at[pl.ds(pl.multiple_of(i * rows, rows), rows)], out_sem.at[lax.rem(i, 2)])

    def gather(i, carry):
        def row(r, c):
            base = r * 16
            for q in range(16):
                t = i * rows + base + q
                gathered[pl.ds((base + q) * parts, parts), :] = wide[pl.ds(dest_ref[t] * parts, parts), :] * gate_ref[t]
            return c
        lax.fori_loop(0, rows // 16, row, 0)
        @pl.when(i >= 2)
        def _():
            store(i - 2).wait()
        for j in range(parts):
            out_buf[lax.rem(i, 2), :, j * LANES:(j + 1) * LANES] = gathered[pl.ds(j, rows, stride=parts), :].astype(jnp.bfloat16)
        store(i).start()
        return carry

    lax.fori_loop(0, tokens // rows, gather, 0)
    store(tokens // rows - 2).wait()
    store(tokens // rows - 1).wait()

def combine(back, dest, gate):
    slots, width = back.shape
    tokens = dest.shape[0]
    parts = width // LANES
    rows = 512
    smem = pl.BlockSpec(memory_space=pltpu.SMEM)
    hbm = pl.BlockSpec(memory_space=pl.ANY)
    return pl.pallas_call(combine_kernel, name="combine",
        out_shape=jax.ShapeDtypeStruct((tokens, width), jnp.bfloat16),
        in_specs=[smem, smem, hbm], out_specs=hbm,
        scratch_shapes=[pltpu.VMEM((slots * parts + 8, LANES), jnp.float32), pltpu.VMEM((rows * parts, LANES), jnp.float32),
            pltpu.VMEM((4, rows, width), jnp.bfloat16), pltpu.VMEM((2, rows, width), jnp.bfloat16),
            pltpu.SemaphoreType.DMA((4,)), pltpu.SemaphoreType.DMA((2,))],
        compiler_params=pltpu.CompilerParams(vmem_limit_bytes=60 * 1024 * 1024))(dest, gate, back)


def solution(mesh):
    nb, na = mesh.shape["ep_b"], mesh.shape["ep_a"]
    num_experts = nb * na
    tok_spec = P(("dp",) + EXPERT_AXES)
    expert_spec = P(EXPERT_AXES)

    def device_step(tokens, expert_ids, route_order, w_route, expert_keys, tau, w_in, b_in, w_out, b_out):
        tok_dev, model_width = tokens.shape[1], tokens.shape[2]
        capacity = (5 * tok_dev + 4 * num_experts - 1) // (4 * num_experts)
        slot_source, dest_slot = route_slots(expert_ids[0], route_order[0], num_experts, capacity)
        returned, gate = exchange(tokens[0], expert_ids[0], slot_source, w_route, expert_keys, tau,
                                  w_in[0], b_in[0], w_out[0], b_out[0], nb, na)
        return combine(returned, dest_slot, gate)[None]

    return jax.shard_map(
        device_step,
        mesh=mesh,
        in_specs=(tok_spec, tok_spec, tok_spec, P(), P(), P(), expert_spec, expert_spec, expert_spec, expert_spec),
        out_specs=tok_spec,
        check_vma=False,
    )
```

time: 551 us -> 471 us (0.85)
  the two profiles are of different devices: /device:TPU:120 before, /device:TPU:105 now
where the time goes in v2:
time: 471 us; the launch traced here: 470 us
  Pallas kernels  454 us (96%)
  other arithmetic  7.99 us (2%)
    pallas_call x1, Pallas kernels, exchange(): pl.pallas_call(functools.partial(exchange_kernel, order, nb, nx), name='e...  428 us
    pallas_call x1, Pallas kernels, combine(): pl.pallas_call(combine_kernel, name='combine', out_shape=jax.ShapeDtypeSt...  26.2 us

profile of v2, /device:TPU:105, one launch (start us, length us, event | category | flops | bytes accessed | tf_op | source)
XLA Modules:
  0.0 470.4 jit_solution(13123283953287933709)
XLA Ops:
  0.7 1.3 convert_element_type.120.b2_ref
  1.9 1.3 convert_element_type.119.b1_ref
  3.2 0.8 convert_reduce_fusion
  4.1 0.8 fusion.36
  4.9 1.3 fusion.13
  6.2 1.9 copy.22
  8.2 0.4 convolution_bitcast_fusion
  8.5 0.2 slice.20
  8.7 0.3 copy.20
  9.0 0.3 copy.21
  9.3 0.4 subtract_reduce_fusion
  9.7 0.4 multiply_reduce_fusion
  10.1 1.7 fusion.9
  11.8 1.4 fusion.15
  13.2 0.6 fusion.27.source_ref
  13.8 1.4 fusion.18
  15.2 0.6 fusion.28.dest_ref
  15.9 428.2 %exchange_mlp.1 = (bf16[32,320,768]{2,1,0:T(8,128)(2,1)}, bf16[32,320,768]{2,1,0:T(8,128)(2,1)}, f32[1,8192]{1,0:T(1,128)}) custom-call(s32[10240]{0:T(1024)} %fusion.27.source_ref, s32[1,8192]{1,0:T(1,128)} %ids_ref.1, f32[1,1]{1,0:T(1,128)} %bitcast.25.tau_ref, bf16[8192,768]{1,0:T(8,128)(2,1)} %bitcast.31, bf16[256,768]{1,0:T(8,128)(2,1)} %bitcast.27, ...), custom_call_target="tpu_custom_call" | custom-call | flops 96636764160 | bytes 47185920 | tf_op jit(solution)/shard_map/exchange_mlp/pallas_call | solution.py:271
  444.1 26.2 %combine.1 = bf16[8192,768]{1,0:T(8,128)(2,1)} custom-call(s32[8192]{0:T(1024)} %fusion.28.dest_ref, f32[8192]{0:T(1024)} %bitcast.29, bf16[10240,768]{1,0:T(8,128)(2,1)} %bitcast.26), custom_call_target="tpu_custom_call" | custom-call | tf_op jit(solution)/shard_map/combine/pallas_call | solution.py:352
  (6 shorter events, 0.1 us)

commit v3 on v2

--- a/solution.py
+++ b/solution.py
@@ -52,22 +52,16 @@
 
 
 def send_order(nb, nx):
-    rest = [(y, x) for y in range(nb) for x in range(nx) if (y, x) != (0, 0)]
-
-    def phase(off):
-        y, x = off
-        near = lambda v, n: v in (1, n - 1)
-        if x == 0 or y == 0:
-            return 0 if near(x, nx) or near(y, nb) else 3
-        if near(x, nx) and near(y, nb):
-            return 1 if (x == 1) == (y == 1) else 2
-        return 4 if not near(x, nx) and not near(y, nb) else 5
-
-    rest.sort(key=phase)
-    out = [(0, 0, 0), (0, 0, 1)]
-    for p in range(6):
-        out += [(y, x, c) for c in range(2) for (y, x) in rest if phase((y, x)) == p]
-    return out
+    near = lambda y, x: [(y, x), ((nb - y) % nb, (nx - x) % nx)]
+    pair = lambda offs, c: [(y, x, c) for y, x in offs]
+    far = lambda y, x: [(y, x, 0), (y, x, 1)]
+    hy, hx = nb // 2, nx // 2
+    col, row = near(1, 0), near(0, 1)
+    same, cross = near(1, 1), near(1, nx - 1)
+    x_one, y_one = near(hy, 1), near(1, hx)
+    return ([(0, 0, 0), (0, 0, 1)] + pair(col, 0) + pair(same, 0) + pair(col, 1) + pair(same, 1) + far(hy, 0)
+            + pair(cross, 0) + pair(cross, 1) + pair(x_one, 0) + pair(row, 0) + pair(x_one, 1) + pair(row, 1)
+            + far(0, hx) + pair(y_one, 0) + pair(y_one, 1) + far(hy, hx))
 
 
 def exchange_kernel(order, nb, nx, source_ref, ids_ref, tau_ref, tok_hbm, wr_ref, key_ref, w1_hbm, b1_ref, w2_hbm, b2_ref,
@@ -159,24 +153,33 @@
             src_ref=a_buf.at[k], dst_ref=r_ref.at[me], send_sem=send2.at[k], recv_sem=recv2.at[k],
             device_id={"ep_b": pb, "ep_a": pa}, device_id_type=MESH)
 
+    def turn(step):
+        return step + jnp.where((step // 4) == 2, row_c * (1 - 2 * lax.rem(step, 2)), 0)
+
+    def seq(i):
+        return jnp.where(i < 2, i, 2 * turn(i // 2) + lax.rem(i + row_c, 2))
+
     pl.semaphore_wait(barrier, count - 1)
 
-    def fill_step(k, carry):
+    def fill_step(i, carry):
+        k = seq(i)
         y, x, c = offset(k)
         pb, pa = peer(y, x, c)
-        slot = lax.rem(k, 2)
+        slot = lax.rem(i, 2)
         fill(pb * (2 * nx) + pa, slot)
         stage_copy(k, slot).start()
 
-        @pl.when(k > 1)
-        def _():
-            stage_copy(k - 1, 1 - slot).wait()
-            send_copy(k - 1).start()
+        @pl.when(i > 1)
+        def _():
+            before = seq(i - 1)
+            stage_copy(before, 1 - slot).wait()
+            send_copy(before).start()
         return carry
 
     lax.fori_loop(1, count, fill_step, 0)
-    stage_copy(count - 1, (count - 1) % 2).wait()
-    send_copy(count - 1).start()
+    last = seq(count - 1)
+    stage_copy(last, (count - 1) % 2).wait()
+    send_copy(last).start()
     fill(me, 0)
     own_in = pltpu.make_async_copy(stage.at[0], s_ref.at[me], lsem.at[0])
     own_in.start()
@@ -192,35 +195,42 @@
         x = a_buf[pl.ds(pair * 2, 2)].reshape(rows, width)
         for n in range(hidden // n1):
             cols = pl.ds(n * n1, n1)
-            part = jnp.dot(x, w1_v[:, cols], preferred_element_type=jnp.float32) + b1_ref[:, cols]
+            part = jnp.dot(x, w1_v[:, cols], preferred_element_type=jnp.float32) + b1_ref[:, cols].astype(jnp.float32)
             part = 0.5 * part * (1.0 + lax.erf(part * 0.7071067811865476))
             h_buf[n // per, :, (n % per) * n1:(n % per + 1) * n1] = part.astype(jnp.bfloat16)
         for n in range(0, width, n2):
             h = jnp.concatenate([h_buf[q] for q in range(depth)], axis=1)
-            y = jnp.dot(h, w2_v[:, n:n + n2], preferred_element_type=jnp.float32) + b2_ref[:, n:n + n2]
+            y = jnp.dot(h, w2_v[:, n:n + n2], preferred_element_type=jnp.float32) + b2_ref[:, n:n + n2].astype(jnp.float32)
             a_buf[pl.ds(pair * 2, 2), :, n:n + n2] = y.astype(jnp.bfloat16).reshape(2, capacity, n2)
 
     own_in.wait()
     w1_copy.wait()
     w2_copy.wait()
 
-    def loop_step(pair, carry):
-        @pl.when(pair > 0)
+    def loop_step(step, carry):
+        pair = turn(step)
+
+        @pl.when(step > 0)
         def _():
             send_copy(2 * pair).wait_recv()
         send_copy(2 * pair + 1).wait_recv()
         mlp(pair)
 
-        @pl.when(pair > 0)
-        def _():
-            back_copy(2 * pair).start()
-        back_copy(2 * pair + 1).start()
+        @pl.when(step > 0)
+        def _():
+            back_copy(2 * pair + row_c).start()
+            back_copy(2 * pair + 1 - row_c).start()
+
+        @pl.when(step == 0)
+        def _():
+            back_copy(1).start()
         return carry
 
     lax.fori_loop(0, count // 2, loop_step, 0)
     own_out = pltpu.make_async_copy(a_buf.at[0], r_ref.at[me], lsem.at[1])
     own_out.start()
 
+    route_t = jnp.transpose(wr_ref[...].astype(jnp.float32)).astype(jnp.bfloat16)
     key = key_ref[...].astype(jnp.float32)
     key_unit = key / jnp.sqrt(jnp.sum(key * key, axis=1, keepdims=True))
     for i in range(depth - 1):
@@ -232,7 +242,7 @@
             token_load(i + depth - 1).start()
         token_load(i).wait()
         x = h_buf[lax.rem(i, depth), pl.ds(0, chunk), :]
-        proj = lax.dot_general(wr_ref[...], x, (((1,), (1,)), ((), ())), preferred_element_type=jnp.float32)
+        proj = lax.dot_general(route_t, x, (((1,), (1,)), ((), ())), preferred_element_type=jnp.float32)
         unit = proj / jnp.sqrt(jnp.sum(proj * proj, axis=0, keepdims=True))
         logits = jnp.dot(key_unit, unit, precision=lax.Precision.HIGHEST, preferred_element_type=jnp.float32) / tau_ref[0, 0]
         weight = jnp.exp(logits - jnp.max(logits, axis=0, keepdims=True))
@@ -287,8 +297,8 @@
         cost_estimate=pl.CostEstimate(flops=flops, bytes_accessed=6 * count * capacity * width, transcendentals=0),
         compiler_params=pltpu.CompilerParams(
             collective_id=0, has_side_effects=True, vmem_limit_bytes=67000000),
-    )(slot_source, id_row[None], tau.reshape(1, 1), tokens, w_route.T, expert_keys,
-      w_first, b_first.astype(jnp.float32)[None], w_second, b_second.astype(jnp.float32)[None])
+    )(slot_source, id_row[None], tau.reshape(1, 1), tokens, w_route, expert_keys,
+      w_first, b_first[None], w_second, b_second[None])
     return returned.reshape(count * capacity, width), gate.reshape(tok_dev)
 
 
@@ -324,12 +334,12 @@
 
     def gather(i, carry):
         def row(r, c):
-            base = r * 16
-            for q in range(16):
+            base = r * 64
+            for q in range(64):
                 t = i * rows + base + q
                 gathered[pl.ds((base + q) * parts, parts), :] = wide[pl.ds(dest_ref[t] * parts, parts), :] * gate_ref[t]
             return c
-        lax.fori_loop(0, rows // 16, row, 0)
+        lax.fori_loop(0, rows // 64, row, 0)
         @pl.when(i >= 2)
         def _():
             store(i - 2).wait()
@@ -346,7 +356,7 @@
     slots, width = back.shape
     tokens = dest.shape[0]
     parts = width // LANES
-    rows = 512
+    rows = 1024
     smem = pl.BlockSpec(memory_space=pltpu.SMEM)
     hbm = pl.BlockSpec(memory_space=pl.ANY)
     return pl.pallas_call(combine_kernel, name="combine",

time: 471 us -> 411 us (0.87)
  Pallas kernels: 454 us -> 399 us
    pallas_call x1, Pallas kernels: 428 us -> 376 us  [exchange(): pl.pallas_call(functools.partial(exchange_kernel, order, nb, nx), name='e...]
where the time goes in v3:
time: 411 us; the launch traced here: 410 us
  Pallas kernels  399 us (97%)
  other arithmetic  5.4 us (1%)
  matrix products  4.46 us (1%)
    pallas_call x1, Pallas kernels, exchange(): pl.pallas_call(functools.partial(exchange_kernel, order, nb, nx), name='e...  376 us
    pallas_call x1, Pallas kernels, combine(): pl.pallas_call(combine_kernel, name='combine', out_shape=jax.ShapeDtypeSt...  22.7 us

profile of v3, /device:TPU:105, one launch (start us, length us, event | category | flops | bytes accessed | tf_op | source)
XLA Modules:
  0.0 410.0 jit_solution(4545728490985097867)
XLA Ops:
  0.7 0.8 convert_reduce_fusion
  1.5 0.8 fusion.36
  2.3 1.3 fusion.13
  3.6 0.4 convolution_bitcast_fusion
  4.0 0.2 slice.20
  4.2 0.3 copy.17
  4.5 0.3 copy.18
  4.8 0.4 subtract_reduce_fusion
  5.2 0.4 multiply_reduce_fusion
  5.6 1.7 fusion.9
  7.3 1.4 fusion.15
  8.7 0.6 fusion.27.source_ref
  9.3 1.4 fusion.18
  10.7 0.6 fusion.28.dest_ref
  11.3 375.8 %exchange_mlp.1 = (bf16[32,320,768]{2,1,0:T(8,128)(2,1)}, bf16[32,320,768]{2,1,0:T(8,128)(2,1)}, f32[1,8192]{1,0:T(1,128)}) custom-call(s32[10240]{0:T(1024)} %fusion.27.source_ref, s32[1,8192]{1,0:T(1,128)} %ids_ref.1, f32[1,1]{1,0:T(1,128)} %bitcast.24.tau_ref, bf16[8192,768]{1,0:T(8,128)(2,1)} %bitcast.29, bf16[768,256]{1,0:T(8,128)(2,1)} %wr_ref.1, ...), custom_call_target="tpu_custom_call" | custom-call | flops 96636764160 | bytes 47185920 | tf_op jit(solution)/shard_map/exchange_mlp/pallas_call | solution.py:281
  387.2 22.7 %combine.1 = bf16[8192,768]{1,0:T(8,128)(2,1)} custom-call(s32[8192]{0:T(1024)} %fusion.28.dest_ref, f32[8192]{0:T(1024)} %bitcast.27, bf16[10240,768]{1,0:T(8,128)(2,1)} %bitcast.25), custom_call_target="tpu_custom_call" | custom-call | tf_op jit(solution)/shard_map/combine/pallas_call | solution.py:362
  (6 shorter events, 0.1 us)

commit v4 on v3

--- a/solution.py
+++ b/solution.py
@@ -59,9 +59,7 @@
     col, row = near(1, 0), near(0, 1)
     same, cross = near(1, 1), near(1, nx - 1)
     x_one, y_one = near(hy, 1), near(1, hx)
-    return ([(0, 0, 0), (0, 0, 1)] + pair(col, 0) + pair(same, 0) + pair(col, 1) + pair(same, 1) + far(hy, 0)
-            + pair(cross, 0) + pair(cross, 1) + pair(x_one, 0) + pair(row, 0) + pair(x_one, 1) + pair(row, 1)
-            + far(0, hx) + pair(y_one, 0) + pair(y_one, 1) + far(hy, hx))
+    return ([(0, 0, 0), (0, 0, 1)] + pair(col, 0) + pair(col, 1) + far(hy, 0) + pair(same, 0) + pair(same, 1) + pair(cross, 0) + pair(cross, 1) + pair(x_one, 0) + pair(row, 0) + pair(x_one, 1) + pair(row, 1) + far(0, hx) + pair(y_one, 0) + pair(y_one, 1) + far(hy, hx))
 
 
 def exchange_kernel(order, nb, nx, source_ref, ids_ref, tau_ref, tok_hbm, wr_ref, key_ref, w1_hbm, b1_ref, w2_hbm, b2_ref,
@@ -128,7 +126,7 @@
         def rows16(r, carry):
             for q in range(16):
                 src = source_ref[block * capacity + r * 16 + q]
-                gathered[pl.ds((r * 16 + q) * parts, parts), :] = wide[pl.ds(src * parts, parts), :]
+                gathered[pl.ds((r * 16 + q) * parts, parts), :] = wide[pl.ds(src, parts), :]
             return carry
         lax.fori_loop(0, capacity // 16, rows16, 0)
         for j in range(parts):
@@ -297,7 +295,7 @@
         cost_estimate=pl.CostEstimate(flops=flops, bytes_accessed=6 * count * capacity * width, transcendentals=0),
         compiler_params=pltpu.CompilerParams(
             collective_id=0, has_side_effects=True, vmem_limit_bytes=67000000),
-    )(slot_source, id_row[None], tau.reshape(1, 1), tokens, w_route, expert_keys,
+    )(slot_source * (width // LANES), id_row[None], tau.reshape(1, 1), tokens, w_route, expert_keys,
       w_first, b_first[None], w_second, b_second[None])
     return returned.reshape(count * capacity, width), gate.reshape(tok_dev)
 
@@ -337,7 +335,7 @@
             base = r * 64
             for q in range(64):
                 t = i * rows + base + q
-                gathered[pl.ds((base + q) * parts, parts), :] = wide[pl.ds(dest_ref[t] * parts, parts), :] * gate_ref[t]
+                gathered[pl.ds((base + q) * parts, parts), :] = wide[pl.ds(dest_ref[t], parts), :] * gate_ref[t]
             return c
         lax.fori_loop(0, rows // 64, row, 0)
         @pl.when(i >= 2)
@@ -365,7 +363,7 @@
         scratch_shapes=[pltpu.VMEM((slots * parts + 8, LANES), jnp.float32), pltpu.VMEM((rows * parts, LANES), jnp.float32),
             pltpu.VMEM((4, rows, width), jnp.bfloat16), pltpu.VMEM((2, rows, width), jnp.bfloat16),
             pltpu.SemaphoreType.DMA((4,)), pltpu.SemaphoreType.DMA((2,))],
-        compiler_params=pltpu.CompilerParams(vmem_limit_bytes=60 * 1024 * 1024))(dest, gate, back)
+        compiler_params=pltpu.CompilerParams(vmem_limit_bytes=60 * 1024 * 1024))(dest * parts, gate, back)
 
 
 def solution(mesh):

time: 411 us -> 408 us (level)
  no operation moved by 1% of the time
where the time goes in v4:
time: 408 us; the launch traced here: 406 us
  Pallas kernels  395 us (97%)
  other arithmetic  5.41 us (1%)
  matrix products  4.46 us (1%)
    pallas_call x1, Pallas kernels, exchange(): pl.pallas_call(functools.partial(exchange_kernel, order, nb, nx), name='e...  374 us
    pallas_call x1, Pallas kernels, combine(): pl.pallas_call(combine_kernel, name='combine', out_shape=jax.ShapeDtypeSt...  20.6 us

profile of v4, /device:TPU:105, one launch (start us, length us, event | category | flops | bytes accessed | tf_op | source)
XLA Modules:
  0.0 406.4 jit_solution(4049760199805942424)
XLA Ops:
  0.7 0.8 convert_reduce_fusion
  1.5 0.8 fusion.38
  2.3 1.3 fusion.13
  3.6 0.4 convolution_bitcast_fusion
  4.0 0.2 slice.20
  4.2 0.3 copy.17
  4.5 0.3 copy.18
  4.8 0.4 subtract_reduce_fusion
  5.2 0.4 multiply_reduce_fusion
  5.6 1.7 fusion.9
  7.3 1.4 fusion.15
  8.7 0.6 fusion.28.source_ref
  9.3 1.4 fusion.18
  10.7 0.6 fusion.30.dest_ref
  11.4 374.3 %exchange_mlp.1 = (bf16[32,320,768]{2,1,0:T(8,128)(2,1)}, bf16[32,320,768]{2,1,0:T(8,128)(2,1)}, f32[1,8192]{1,0:T(1,128)}) custom-call(s32[10240]{0:T(1024)} %fusion.28.source_ref, s32[1,8192]{1,0:T(1,128)} %ids_ref.1, f32[1,1]{1,0:T(1,128)} %bitcast.24.tau_ref, bf16[8192,768]{1,0:T(8,128)(2,1)} %bitcast.29, bf16[768,256]{1,0:T(8,128)(2,1)} %wr_ref.1, ...), custom_call_target="tpu_custom_call" | custom-call | flops 96636764160 | bytes 47185920 | tf_op jit(solution)/shard_map/exchange_mlp/pallas_call | solution.py:279
  385.7 20.6 %combine.1 = bf16[8192,768]{1,0:T(8,128)(2,1)} custom-call(s32[8192]{0:T(1024)} %fusion.30.dest_ref, f32[8192]{0:T(1024)} %bitcast.27, bf16[10240,768]{1,0:T(8,128)(2,1)} %bitcast.25), custom_call_target="tpu_custom_call" | custom-call | tf_op jit(solution)/shard_map/combine/pallas_call | solution.py:360
  (6 shorter events, 0.1 us)
